TPU v7x, 32 devices: a whole 2x2x4 slice. The times are simulated.
32 devices in a mesh: groups: 2 (over y), seq: 4 (over z), exp: 2 (over x), rep: 2 (over core).
Axes of the slice: x: 2, y: 2, z: 4, core: 2. Of those that a mesh axis runs over, the one named last changes fastest.
Arguments:
- queries: bfloat16 [512, 4096], P(('groups', 'seq'), ('exp', 'rep')), parts along dimension 0, may hold values from -4 to 4
- key_rows: bfloat16 [512, 4096], P(('groups', 'seq'), ('exp', 'rep')), parts along dimension 0, may hold values from -4 to 4
- value_rows: bfloat16 [512, 4096], P(('groups', 'seq'), ('exp', 'rep')), parts along dimension 0, may hold values from -6 to 6
- decay_log: float32 [512, 32], P(('groups', 'seq'), ('exp', 'rep')), parts along dimension 0, may hold values from -1.5 to 0
- residual: bfloat16 [512, 4096], P(('groups', 'seq'), ('exp', 'rep')), parts along dimension 0, may hold values from -6 to 6
- out_gate: bfloat16 [512, 4096], P(('groups', 'seq'), ('exp', 'rep')), parts along dimension 0, may hold values from -6 to 6
- attn_gain: float32 [4096], P(('exp', 'rep')), may hold values from 0.1 to 1.9
- moe_gain: float32 [4096], P(('exp', 'rep')), may hold values from 0.1 to 1.9
- routes: int32 [512, 2], P(('groups', 'seq')), parts along dimension 0, may hold values from 0 to 31, as said below
- route_weights: float32 [512, 2], P(('groups', 'seq')), parts along dimension 0, may hold values from 0.3 to 1
- w_gate: bfloat16 [2, 4608, 4096], P('exp', 'seq'), may hold values from -0.09375 to 0.09375
- w_up: bfloat16 [2, 4608, 4096], P('exp', 'seq'), may hold values from -0.09375 to 0.09375
- w_down: bfloat16 [2, 4608, 4096], P('exp', 'seq'), may hold values from -0.09375 to 0.09375
Outputs:
- layer_out: bfloat16 [512, 4096], P(('groups', 'seq'), ('exp', 'rep')), parts along dimension 0
There are 2 independent parts, one for each index of `groups`. A program takes and returns all parts, laid end to end along the dimension named above; an argument that names none is the same for every part. Nothing has to cross between parts.
Inputs may be any that keep to these rules, and one draw needn't show every extreme that they name: `routes`: each row names two different experts. Within each aligned block of 64 rows no expert is named by more than 6 rows, every expert is named in every block, and one expert below 2 is named by exactly 6 rows in every block.
All inputs are finite; a program needn't handle non-finite values.
Results may differ from a plain program's by a relative error of at most 0.01.
Values may be sent and summed in bfloat16 or wider, within the bound.
A program may use at most 64 MiB of HBM per device.

v0:
```python
import jax
import jax.numpy as jnp
from jax import lax
from jax.experimental import pallas as pl
from jax.experimental.pallas import tpu as pltpu
from jax.sharding import PartitionSpec as P

CAP = 6
SLOTS = 8
PARTS = 2
EPSILON = 1e-06
MESH = pl.DeviceIdType.MESH
F32 = jnp.float32
BF16 = jnp.bfloat16


def sweep(count, body):
    if count <= 16:
        for i in range(count):
            body(i)
    else:
        lax.fori_loop(0, count, lambda i, c: (body(i), c)[1], 0)


def nt_dot(a, b):
    return lax.dot_general(a, b, (((1,), (1,)), ((), ())), preferred_element_type=F32)


def kernel(
    n_seq,
    n_exp,
    n_rep,
    k_hbm,
    v_hbm,
    decay_hbm,
    q_hbm,
    routes_hbm,
    rw_hbm,
    res_hbm,
    gate_hbm,
    again_hbm,
    mgain_hbm,
    wg_hbm,
    wu_hbm,
    wd_hbm,
    out_ref,
    k_ref,
    v_ref,
    decay_ref,
    q_ref,
    routes_ref,
    rw_ref,
    res_ref,
    gate_ref,
    again_ref,
    mgain_ref,
    wg,
    wu,
    wd,
    state_in,
    state_out,
    block_state,
    att,
    u_buf,
    sums,
    pack,
    rows,
    half_send,
    half_recv,
    fin,
    back,
    in_sem,
    w_sem,
    go_sem,
    chain_send,
    chain_recv,
    sums_send,
    sums_recv,
    disp_send,
    disp_recv,
    swap_send,
    swap_recv,
    half_ssem,
    half_rsem,
    back_send,
    back_recv,
):
    z = lax.axis_index("seq")
    x = lax.axis_index("exp")
    r = lax.axis_index("rep")
    other = 1 - r
    tokens, columns = q_ref.shape
    heads = decay_ref.shape[0]
    hd = columns // heads
    part_rows = hd // PARTS
    hidden_rows = wg.shape[0]
    width = columns * n_exp * n_rep
    whole_rows = wg_hbm.shape[1]

    inputs = [
        pltpu.make_async_copy(src, dst, in_sem.at[i])
        for i, (src, dst) in enumerate(
            (
                (k_hbm, k_ref),
                (v_hbm, v_ref),
                (decay_hbm, decay_ref),
                (q_hbm, q_ref),
                (routes_hbm, routes_ref),
                (rw_hbm, rw_ref),
                (res_hbm, res_ref),
                (gate_hbm, gate_ref),
                (again_hbm, again_ref),
                (mgain_hbm, mgain_ref),
            )
        )
    ]
    for load in inputs:
        load.start()
    first = pl.multiple_of(r * hidden_rows, 16) if hidden_rows != whole_rows else 0
    loads = [
        pltpu.make_async_copy(src.at[0, pl.ds(first, hidden_rows), :], dst, w_sem.at[i])
        for i, (src, dst) in enumerate(((wg_hbm, wg), (wu_hbm, wu), (wd_hbm, wd)))
    ]

    barrier = pltpu.get_barrier_semaphore()
    plane = n_exp * n_seq
    peers = n_exp * n_rep
    me = x * n_rep + r
    last = n_seq - 1

    def greet(where):
        pl.semaphore_signal(barrier, inc=1, device_id=where, device_id_type=MESH)

    @pl.when(z < last)
    def _():
        greet({"seq": z + 1})

    @pl.when(z > 0)
    def _():
        greet({"seq": z - 1})

    def greet_peer(i):
        to = lax.rem(me + 1 + i, peers)
        greet({"exp": lax.div(to, n_rep), "rep": lax.rem(to, n_rep)})

    sweep(peers - 1, greet_peer)
    for load in loads:
        load.start()
    for load in inputs[:3]:
        load.wait()

    ti = lax.broadcasted_iota(jnp.int32, (tokens, tokens), 0)
    tj = lax.broadcasted_iota(jnp.int32, (tokens, tokens), 1)
    causal = ti >= tj
    upper = jnp.where(tj >= ti, 1.0, 0.0).astype(F32)
    cum_t = jnp.dot(
        decay_ref[...], upper, precision=lax.Precision.HIGHEST, preferred_element_type=F32
    )
    cum = jnp.transpose(cum_t)
    ending = cum[tokens - 1 : tokens, :]
    fading = jnp.exp(ending)
    to_end = jnp.exp(ending - cum)
    lift = jnp.exp(cum)
    for h in range(heads):
        cols = slice(h * hd, (h + 1) * hd)
        faded = k_ref[:, cols].astype(F32) * to_end[:, h : h + 1]
        block_state[h] = jnp.dot(
            jnp.transpose(faded).astype(BF16), v_ref[:, cols], preferred_element_type=F32
        )

    ends = (z > 0).astype(jnp.int32) + (z < last).astype(jnp.int32)
    pl.semaphore_wait(barrier, peers - 1 + ends)

    def hop(h, p):
        piece = pl.ds(p * part_rows, part_rows)
        return pltpu.make_async_remote_copy(
            src_ref=state_out.at[h, piece],
            dst_ref=state_in.at[h, piece],
            send_sem=chain_send.at[h, p],
            recv_sem=chain_recv.at[h, p],
            device_id={"seq": z + 1},
            device_id_type=MESH,
        )

    @pl.when(z == 0)
    def _():
        for h in range(heads):
            state_out[h] = block_state[h].astype(BF16)
            for p in range(PARTS):
                hop(h, p).start()

    inputs[3].wait()

    for h in range(heads):
        cols = slice(h * hd, (h + 1) * hd)
        scores = nt_dot(q_ref[:, cols], k_ref[:, cols])
        gaps = cum[:, h : h + 1] - cum_t[h : h + 1, :]
        mixing = jnp.where(causal, scores * jnp.exp(jnp.where(causal, gaps, 0.0)), 0.0)
        att[:, cols] = jnp.dot(mixing.astype(BF16), v_ref[:, cols], preferred_element_type=F32)

    for load in inputs[4:]:
        load.wait()
    lane = lax.broadcasted_iota(jnp.int32, (tokens, 128), 1)
    expert_of = lax.div(lane, SLOTS)
    slot_of = lax.rem(lane, SLOTS)
    named = jnp.transpose(routes_ref[...].astype(F32)).astype(jnp.int32)
    shares = jnp.transpose(rw_ref[...])
    first_hit = named[:, 0:1] == expert_of
    second_hit = named[:, 1:2] == expert_of
    hit = jnp.where(first_hit | second_hit, 1.0, 0.0)
    strict = jnp.where(ti > tj, 1.0, 0.0).astype(BF16)
    before = jnp.dot(strict, hit.astype(BF16), preferred_element_type=F32)
    taken = (hit > 0.5) & (before.astype(jnp.int32) == slot_of) & (slot_of < CAP)
    onehot = jnp.where(taken, 1.0, 0.0)
    combine = jnp.where(first_hit, shares[:, 0:1], shares[:, 1:2]) * onehot
    dispatch = jnp.transpose(onehot)[0 : n_exp * SLOTS, :].astype(BF16)

    def let_go(i):
        pl.semaphore_signal(go_sem, inc=1, device_id={"seq": i}, device_id_type=MESH)

    for h in range(heads):
        cols = slice(h * hd, (h + 1) * hd)

        @pl.when(z > 0)
        def _():
            for p in range(PARTS):
                piece = slice(p * part_rows, (p + 1) * part_rows)
                hop(h, p).wait_recv()

                @pl.when(z < last)
                def _():
                    state_out[h, piece] = (
                        fading[:, h : h + 1] * state_in[h, piece].astype(F32)
                        + block_state[h, piece]
                    ).astype(BF16)
                    hop(h, p).start()

            lifted = (q_ref[:, cols].astype(F32) * lift[:, h : h + 1]).astype(BF16)
            att[:, cols] += jnp.dot(lifted, state_in[h], preferred_element_type=F32)

        if h == max(heads - 3, 0):

            @pl.when(z == last)
            def _():
                sweep(last, let_go)

    res = res_ref[...].astype(F32)
    attended = att[...]
    u = jax.nn.sigmoid(gate_ref[...].astype(F32)) * attended * again_ref[...]
    u_buf[...] = u
    parts = (attended * attended, res * u, u * u, res * res)
    table = jnp.zeros((tokens, 128), F32)
    for i, part in enumerate(parts):
        table = jnp.where(lane == i, jnp.sum(part, axis=1, keepdims=True), table)
    sums[me] = jnp.transpose(table)[0:8, :]

    def tell(i):
        to = lax.rem(me + 1 + i, peers)
        pltpu.make_async_remote_copy(
            src_ref=sums.at[me],
            dst_ref=sums.at[me],
            send_sem=sums_send,
            recv_sem=sums_recv,
            device_id={"exp": lax.div(to, n_rep), "rep": lax.rem(to, n_rep)},
            device_id_type=MESH,
        ).start()

    sweep(peers - 1, tell)
    many = sums.at[pl.ds(0, peers - 1)]
    pltpu.make_async_copy(many, many, sums_recv).wait()
    total = jnp.sum(sums[...], axis=0)
    s1 = lax.rsqrt(total[0:1, :] / width + EPSILON)
    moe = total[3:4, :] + s1 * (2.0 * total[1:2, :] + s1 * total[2:3, :])
    s2 = lax.rsqrt(jnp.maximum(moe, 0.0) / width + EPSILON)
    row8 = lax.broadcasted_iota(jnp.int32, (8, tokens), 0)
    scales = jnp.transpose(jnp.where(row8 == 0, s1, s2))
    hidden = res_ref[...].astype(F32) + scales[:, 0:1] * u_buf[...]
    u_buf[...] = hidden
    normed = (hidden * scales[:, 1:2] * mgain_ref[...]).astype(BF16)

    packed = jnp.dot(dispatch, normed, preferred_element_type=F32)
    for e in range(n_exp):
        pack[e] = packed[e * SLOTS : (e + 1) * SLOTS, :].astype(BF16)
    here = x * n_seq + z
    rows[r, here] = pack[x]

    def deal(e, to, source, target, send_sem, recv_sem):
        pltpu.make_async_remote_copy(
            src_ref=source,
            dst_ref=target,
            send_sem=send_sem,
            recv_sem=recv_sem,
            device_id={"exp": e, "seq": to},
            device_id_type=MESH,
        ).start()

    def deal_rows(e, to):
        used = pl.ds(0, CAP)
        deal(e, to, pack.at[e, used], rows.at[r, here, used], disp_send, disp_recv)

    def earlier(send):
        def one(i):
            @pl.when(i < z)
            def _():
                for e in range(n_exp):
                    send(e, i)

        sweep(n_seq, one)

    def level(send):
        for j in range(1, n_exp):
            send(lax.rem(x + j, n_exp), z)

    def later(send):
        def one(i):
            @pl.when(last - i > z)
            def _():
                for e in range(n_exp):
                    send(e, last - i)

        sweep(n_seq, one)

    earlier(deal_rows)
    level(deal_rows)

    @pl.when(z < last)
    def _():
        pl.semaphore_wait(go_sem, 1)

    later(deal_rows)
    arrived = rows.at[r, pl.ds(0, plane - 1), pl.ds(0, CAP)]
    pltpu.make_async_copy(arrived, arrived, disp_recv).wait()
    swap = pltpu.make_async_remote_copy(
        src_ref=rows.at[r],
        dst_ref=rows.at[r],
        send_sem=swap_send,
        recv_sem=swap_recv,
        device_id={"rep": other},
        device_id_type=MESH,
    )
    swap.start()
    for load in loads:
        load.wait()
    slots = n_seq * SLOTS

    def project(s):
        gate_part = up_part = 0.0
        for e in range(n_exp):
            chunk = rows[s, pl.ds(e * n_seq, n_seq)].astype(F32).reshape(slots, columns)
            chunk = chunk.astype(BF16)
            at = pl.ds(pl.multiple_of((e * n_rep + s) * columns, 128), columns)
            gate_part += nt_dot(wg[:, at], chunk)
            up_part += nt_dot(wu[:, at], chunk)
        return gate_part, up_part

    gate_val, up_val = project(r)
    swap.wait()
    gate_part, up_part = project(other)
    gate_val += gate_part
    up_val += up_part
    inner = gate_val / (1.0 + jnp.exp(-gate_val)) * up_val
    if hidden_rows == whole_rows:
        unit = lax.broadcasted_iota(jnp.int32, inner.shape, 0)
        inner = jnp.where(lax.div(unit, whole_rows // n_rep) == r, inner, 0.0)
    inner = jnp.transpose(inner).astype(BF16)

    def product(e, s):
        at = pl.multiple_of((e * n_rep + s) * columns, 128)
        return jnp.dot(inner, wd[:, pl.ds(at, columns)], preferred_element_type=F32)

    def half(e):
        return pltpu.make_async_remote_copy(
            src_ref=half_send.at[e],
            dst_ref=half_recv.at[e],
            send_sem=half_ssem.at[e],
            recv_sem=half_rsem.at[e],
            device_id={"rep": other},
            device_id_type=MESH,
        )

    for e in range(n_exp):
        half_send[e] = product(e, other).astype(BF16)
        half(e).start()

    here_back = x * n_seq + z
    for e in range(n_exp):
        own = product(e, r)
        half(e).wait_recv()
        whole = (own + half_recv[e].astype(F32)).reshape(n_seq, SLOTS, columns)
        fin[pl.ds(e * n_seq, n_seq)] = whole.astype(BF16)

    back[here_back] = fin[here_back]

    def hand_back(e, to):
        used = pl.ds(0, CAP)
        source = fin.at[e * n_seq + to, used]
        deal(e, to, source, back.at[here_back, used], back_send, back_recv)

    earlier(hand_back)
    later(hand_back)
    level(hand_back)
    returned = back.at[pl.ds(0, plane - 1), pl.ds(0, CAP)]
    pltpu.make_async_copy(returned, returned, back_recv).wait()
    coarse = combine.astype(BF16)
    fine = (combine - coarse.astype(F32)).astype(BF16)
    result = u_buf[...]
    for e in range(n_exp):
        rows_e = jnp.sum(back[pl.ds(e * n_seq, n_seq)].astype(F32), axis=0)
        slot = lax.broadcasted_iota(jnp.int32, rows_e.shape, 0)
        rows_e = jnp.where(slot < CAP, rows_e, 0.0).astype(BF16)
        lanes = slice(e * SLOTS, (e + 1) * SLOTS)
        result += jnp.dot(coarse[:, lanes], rows_e, preferred_element_type=F32)
        result += jnp.dot(fine[:, lanes], rows_e, preferred_element_type=F32)
    out_ref[...] = result.astype(BF16)

    for h in range(heads):

        @pl.when(z < last)
        def _():
            for p in range(PARTS):
                hop(h, p).wait_send()

    pltpu.make_async_copy(many, many, sums_send).wait()
    pltpu.make_async_copy(arrived, arrived, disp_send).wait()
    for e in range(n_exp):
        half(e).wait_send()
    pltpu.make_async_copy(returned, returned, back_send).wait()


def solution(mesh):
    n_seq, n_exp, n_rep = (mesh.shape[a] for a in ("seq", "exp", "rep"))

    def shards(
        queries,
        key_rows,
        value_rows,
        decay_log,
        residual,
        out_gate,
        attn_gain,
        moe_gain,
        routes,
        route_weights,
        w_gate,
        w_up,
        w_down,
    ):
        tokens, columns = queries.shape
        heads = decay_log.shape[1]
        hd = columns // heads
        _, whole_rows, width = w_gate.shape
        even = whole_rows % (16 * n_rep) == 0
        hidden_rows = whole_rows // n_rep if even else whole_rows
        plane = n_exp * n_seq
        slots = n_seq * SLOTS
        vmem = pl.BlockSpec(memory_space=pltpu.VMEM)
        hbm = pl.BlockSpec(memory_space=pltpu.HBM)
        dma = pltpu.SemaphoreType.DMA
        return pl.pallas_call(
            lambda *refs: kernel(n_seq, n_exp, n_rep, *refs),
            name="layer",
            out_shape=jax.ShapeDtypeStruct((tokens, columns), BF16),
            in_specs=[hbm] * 13,
            out_specs=vmem,
            scratch_shapes=[
                pltpu.VMEM((tokens, columns), BF16),
                pltpu.VMEM((tokens, columns), BF16),
                pltpu.VMEM((heads, tokens), F32),
                pltpu.VMEM((tokens, columns), BF16),
                pltpu.VMEM((2, tokens), jnp.int32),
                pltpu.VMEM((2, tokens), F32),
                pltpu.VMEM((tokens, columns), BF16),
                pltpu.VMEM((tokens, columns), BF16),
                pltpu.VMEM((1, columns), F32),
                pltpu.VMEM((1, columns), F32),
                pltpu.VMEM((hidden_rows, width), BF16),
                pltpu.VMEM((hidden_rows, width), BF16),
                pltpu.VMEM((hidden_rows, width), BF16),
                pltpu.VMEM((heads, hd, hd), BF16),
                pltpu.VMEM((heads, hd, hd), BF16),
                pltpu.VMEM((heads, hd, hd), F32),
                pltpu.VMEM((tokens, columns), F32),
                pltpu.VMEM((tokens, columns), F32),
                pltpu.VMEM((n_exp * n_rep, 8, tokens), F32),
                pltpu.VMEM((n_exp, SLOTS, columns), BF16),
                pltpu.VMEM((n_rep, plane, SLOTS, columns), BF16),
                pltpu.VMEM((n_exp, slots, columns), BF16),
                pltpu.VMEM((n_exp, slots, columns), BF16),
                pltpu.VMEM((plane, SLOTS, columns), BF16),
                pltpu.VMEM((plane, SLOTS, columns), BF16),
                dma((10,)),
                dma((3,)),
                pltpu.SemaphoreType.REGULAR,
                dma((heads, PARTS)),
                dma((heads, PARTS)),
                dma,
                dma,
                dma,
                dma,
                dma,
                dma,
                dma((n_exp,)),
                dma((n_exp,)),
                dma,
                dma,
            ],
            compiler_params=pltpu.CompilerParams(collective_id=0, has_side_effects=True),
        )(
            key_rows,
            value_rows,
            decay_log.T,
            queries,
            routes.T,
            route_weights.T,
            residual,
            out_gate,
            attn_gain.reshape(1, columns),
            moe_gain.reshape(1, columns),
            w_gate,
            w_up,
            w_down,
        )

    block = P(("groups", "seq"), ("exp", "rep"))
    gain = P(("exp", "rep"))
    route = P(("groups", "seq"), None)
    weight = P("exp", "seq", None)
    return jax.shard_map(
        shards,
        mesh=mesh,
        in_specs=(block,) * 6 + (gain, gain, route, route) + (weight,) * 3,
        out_specs=block,
        check_vma=False,
    )
```

profile of v0, /device:TPU:0, one launch (start us, length us, event | category | flops | bytes accessed | tf_op | source)
XLA Modules:
  0.0 35.6 jit_solution(2315297453998371589)
XLA Ops:
  0.0 34.1 %layer.1 = bf16[64,1024]{1,0:T(8,128)(2,1)} custom-call(bf16[64,1024]{1,0:T(8,128)(2,1)} %refs_0_.1, bf16[64,1024]{1,0:T(8,128)(2,1)} %refs_1_.1, f32[8,64]{1,0:T(8,128)} %bitcast.5, bf16[64,1024]{1,0:T(8,128)(2,1)} %refs_3_.1, s32[2,64]{1,0:T(2,128)} %bitcast.8, f32[2,64]{1,0:T(2,128)} %bitcast.9, bf16[64,1024]{1,0:T(8,128)(2,1)} %refs_6_.1, ...), custom_call_target="tpu_custom_call" | custom-call | tf_op jit(solution)/shard_map/layer/pallas_call | solution.py:459
  34.1 1.6 %copy.15 = bf16[64,1024]{1,0:T(8,128)(2,1)} copy(bf16[64,1024]{1,0:T(8,128)(2,1)} %layer.1) | data formatting | bytes 262144
where the time goes:
time: 35.8 us; the launch traced here: 35.6 us
  Pallas kernels  34.1 us (95%)
  local copies, waits for them, and re-layouts  1.57 us (4%)
    pallas_call x1, Pallas kernels, shards(): pl.pallas_call(lambda *refs: kernel(n_seq, n_exp, n_rep, *refs), name='la...  34.1 us
    unnamed x1, local copies, waits for them, and re-layouts  1.57 us

commit v1 on v0

--- a/solution.py
+++ b/solution.py
@@ -459,7 +459,7 @@
         return pl.pallas_call(
             lambda *refs: kernel(n_seq, n_exp, n_rep, *refs),
             name="layer",
-            out_shape=jax.ShapeDtypeStruct((tokens, columns), BF16),
+            out_shape=pltpu.VMEM((tokens, columns), BF16),
             in_specs=[hbm] * 13,
             out_specs=vmem,
             scratch_shapes=[
@@ -504,7 +504,7 @@
                 dma,
                 dma,
             ],
-            compiler_params=pltpu.CompilerParams(collective_id=0, has_side_effects=True),
+            compiler_params=pltpu.CompilerParams(collective_id=0, has_side_effects=True, vmem_limit_bytes=63000000),
         )(
             key_rows,
             value_rows,

time: 35.8 us -> 34.2 us (0.955)
  local copies, waits for them, and re-layouts: 1.57 us -> 0.66 us
  Pallas kernels: 34.1 us -> 33.4 us
    unnamed x1, local copies, waits for them, and re-layouts: 1.57 us -> 0.66 us
    pallas_call x1, Pallas kernels: 34.1 us -> 33.4 us  [shards(): pl.pallas_call(lambda *refs: kernel(n_seq, n_exp, n_rep, *refs), name='la...]
where the time goes in v1:
time: 34.2 us; the launch traced here: 34.1 us
  Pallas kernels  33.4 us (98%)
  local copies, waits for them, and re-layouts  0.66 us (2%)
    pallas_call x1, Pallas kernels, shards(): pl.pallas_call(lambda *refs: kernel(n_seq, n_exp, n_rep, *refs), name='la...  33.4 us

profile of v1, /device:TPU:0, one launch (start us, length us, event | category | flops | bytes accessed | tf_op | source)
XLA Modules:
  0.0 34.1 jit_solution(9049089031775780532)
XLA Ops:
  0.0 33.4 %layer.1 = bf16[64,1024]{1,0:T(8,128)(2,1)S(1)} custom-call(bf16[64,1024]{1,0:T(8,128)(2,1)} %refs_0_.1, bf16[64,1024]{1,0:T(8,128)(2,1)} %refs_1_.1, f32[8,64]{1,0:T(8,128)} %bitcast.5, bf16[64,1024]{1,0:T(8,128)(2,1)} %refs_3_.1, s32[2,64]{1,0:T(2,128)} %bitcast.8, f32[2,64]{1,0:T(2,128)} %bitcast.9, bf16[64,1024]{1,0:T(8,128)(2,1)} %refs_6_.1, ...), custom_call_target="tpu_custom_call" | custom-call | tf_op jit(solution)/shard_map/layer/pallas_call | solution.py:459
  33.4 0.7 %copy.15 = bf16[64,1024]{1,0:T(8,128)(2,1)} copy(bf16[64,1024]{1,0:T(8,128)(2,1)S(1)} %layer.1) | data formatting | bytes 262144

commit v2 on v1

--- a/solution.py
+++ b/solution.py
@@ -8,6 +8,7 @@
 CAP = 6
 SLOTS = 8
 PARTS = 2
+SHORT = 4
 EPSILON = 1e-06
 MESH = pl.DeviceIdType.MESH
 F32 = jnp.float32
@@ -26,7 +27,7 @@
     return lax.dot_general(a, b, (((1,), (1,)), ((), ())), preferred_element_type=F32)
 
 
-def kernel(
+def chain_kernel(
     n_seq,
     n_exp,
     n_rep,
@@ -427,6 +428,738 @@
     pltpu.make_async_copy(returned, returned, back_send).wait()
 
 
+def direct_kernel(
+    n_seq,
+    n_exp,
+    n_rep,
+    k_hbm,
+    v_hbm,
+    decay_hbm,
+    q_hbm,
+    routes_hbm,
+    rw_hbm,
+    res_hbm,
+    gate_hbm,
+    again_hbm,
+    mgain_hbm,
+    wg_hbm,
+    wu_hbm,
+    wd_hbm,
+    out_ref,
+    k_ref,
+    v_ref,
+    decay_ref,
+    q_ref,
+    routes_ref,
+    rw_ref,
+    res_ref,
+    gate_ref,
+    again_ref,
+    mgain_ref,
+    wg,
+    wu,
+    wd,
+    state_in,
+    state_out,
+    own_state,
+    block_state,
+    lifted,
+    att,
+    u_buf,
+    sums,
+    first_sums,
+    end_send,
+    end_recv,
+    q_send,
+    q_recv,
+    part_send,
+    part_recv,
+    tail_recv,
+    extra_send,
+    extra_recv,
+    near,
+    acc,
+    res_pack,
+    res_rows,
+    pack,
+    rows,
+    gate_early,
+    up_early,
+    half_send,
+    half_recv,
+    fin,
+    back,
+    in_sem,
+    w_sem,
+    go_sem,
+    chain_send,
+    chain_recv,
+    sums_send,
+    sums_recv,
+    first_ssem,
+    first_rsem,
+    q_ssem,
+    q_rsem,
+    end_ssem,
+    end_rsem,
+    part_ssem,
+    part_rsem,
+    extra_ssem,
+    extra_rsem,
+    res_ssem,
+    res_rsem,
+    disp_send,
+    disp_recv,
+    swap_send,
+    swap_recv,
+    half_ssem,
+    half_rsem,
+    back_send,
+    back_recv,
+):
+    z = lax.axis_index("seq")
+    x = lax.axis_index("exp")
+    r = lax.axis_index("rep")
+    other = 1 - r
+    tokens, columns = q_ref.shape
+    heads = decay_ref.shape[0]
+    hd = columns // heads
+    part_rows = hd // PARTS
+    hidden_rows = wg.shape[0]
+    width = columns * n_exp * n_rep
+    whole_rows = wg_hbm.shape[1]
+    plane = n_exp * n_seq
+    peers = n_exp * n_rep
+    me = x * n_rep + r
+    last = n_seq - 1
+    middle = last // 2
+    picked = n_exp * SLOTS
+    used = pl.ds(0, CAP)
+    here = x * n_seq + z
+
+    def home(b):
+        return b if b < last else middle
+
+    inputs = {
+        name: pltpu.make_async_copy(src, dst, in_sem.at[i])
+        for i, (name, src, dst) in enumerate(
+            (
+                ("decay", decay_hbm, decay_ref),
+                ("routes", routes_hbm, routes_ref),
+                ("q", q_hbm, q_ref),
+                ("k", k_hbm, k_ref),
+                ("v", v_hbm, v_ref),
+                ("res", res_hbm, res_ref),
+                ("gate", gate_hbm, gate_ref),
+                ("again", again_hbm, again_ref),
+                ("mgain", mgain_hbm, mgain_ref),
+                ("rw", rw_hbm, rw_ref),
+            )
+        )
+    }
+    for load in inputs.values():
+        load.start()
+
+    barrier = pltpu.get_barrier_semaphore()
+
+    def greet(where):
+        pl.semaphore_signal(barrier, inc=1, device_id=where, device_id_type=MESH)
+
+    for i in range(n_seq):
+
+        @pl.when((i != z) & ((i > 0) | (z == 1)))
+        def _():
+            greet({"seq": i})
+
+    for i in range(peers - 1):
+        to = lax.rem(me + 1 + i, peers)
+        greet({"exp": lax.div(to, n_rep), "rep": lax.rem(to, n_rep)})
+
+    first = pl.multiple_of(r * hidden_rows, 16) if hidden_rows != whole_rows else 0
+    loads = [
+        pltpu.make_async_copy(src.at[0, pl.ds(first, hidden_rows), :], dst, w_sem.at[i])
+        for i, (src, dst) in enumerate(((wg_hbm, wg), (wu_hbm, wu), (wd_hbm, wd)))
+    ]
+    for load in loads:
+        load.start()
+
+    def remote(src, dst, send_sem, recv_sem, where):
+        return pltpu.make_async_remote_copy(
+            src_ref=src,
+            dst_ref=dst,
+            send_sem=send_sem,
+            recv_sem=recv_sem,
+            device_id=where,
+            device_id_type=MESH,
+        )
+
+    inputs["decay"].wait()
+    ti = lax.broadcasted_iota(jnp.int32, (tokens, tokens), 0)
+    tj = lax.broadcasted_iota(jnp.int32, (tokens, tokens), 1)
+    causal = ti >= tj
+    upper = jnp.where(tj >= ti, 1.0, 0.0).astype(F32)
+    cum_t = jnp.dot(
+        decay_ref[...], upper, precision=lax.Precision.HIGHEST, preferred_element_type=F32
+    )
+    cum = jnp.transpose(cum_t)
+    ending = cum[tokens - 1 : tokens, :]
+    fading = jnp.exp(ending)
+    to_end = jnp.exp(ending - cum)
+    lift = jnp.exp(cum)
+    end_send[...] = jnp.zeros(end_send.shape, F32)
+    end_send[:, 0:heads] = ending
+    inputs["routes"].wait()
+    lane = lax.broadcasted_iota(jnp.int32, (tokens, 128), 1)
+    expert_of = lax.div(lane, SLOTS)
+    slot_of = lax.rem(lane, SLOTS)
+    named = jnp.transpose(routes_ref[...].astype(F32)).astype(jnp.int32)
+    first_hit = named[:, 0:1] == expert_of
+    second_hit = named[:, 1:2] == expert_of
+    hit = jnp.where(first_hit | second_hit, 1.0, 0.0)
+    strict = jnp.where(ti > tj, 1.0, 0.0).astype(BF16)
+    before = jnp.dot(strict, hit.astype(BF16), preferred_element_type=F32)
+    taken = (hit > 0.5) & (before.astype(jnp.int32) == slot_of) & (slot_of < CAP)
+    onehot = jnp.where(taken, 1.0, 0.0)
+    dispatch = jnp.transpose(onehot)[0:picked, :].astype(BF16)
+
+    def pick(values):
+        return jnp.dot(dispatch, values, preferred_element_type=F32)
+
+    def put(ref, values):
+        for e in range(n_exp):
+            ref[e, :, 0:columns] = values[e * SLOTS : (e + 1) * SLOTS, :].astype(BF16)
+
+    def take(ref):
+        return ref[...].astype(F32)[:, :, 0:columns].reshape(picked, columns)
+
+    inputs["q"].wait()
+    for h in range(heads):
+        cols = slice(h * hd, (h + 1) * hd)
+        lifted[:, cols] = (q_ref[:, cols].astype(F32) * lift[:, h : h + 1]).astype(BF16)
+    put(q_send, pick(lifted[...]))
+
+    def keep_state():
+        inputs["k"].wait()
+        inputs["v"].wait()
+        for h in range(heads):
+            cols = slice(h * hd, (h + 1) * hd)
+            faded = k_ref[:, cols].astype(F32) * to_end[:, h : h + 1]
+            state = jnp.dot(
+                jnp.transpose(faded).astype(BF16), v_ref[:, cols], preferred_element_type=F32
+            )
+            block_state[h] = state
+            own_state[h] = state.astype(BF16)
+
+    @pl.when(z < last - 1)
+    def _():
+        keep_state()
+
+    pl.semaphore_wait(barrier, jnp.where(z == 0, 1, last) + peers - 1)
+
+    def let_go():
+        for i in range(1, n_exp):
+            pl.semaphore_signal(
+                go_sem,
+                inc=1,
+                device_id={"exp": lax.rem(x + i, n_exp)},
+                device_id_type=MESH,
+            )
+
+    @pl.when(z > 0)
+    def _():
+        let_go()
+
+
+    def ask(to):
+        where = {"seq": to}
+        return (
+            remote(
+                q_send.at[:, used], q_recv.at[z, :, used], q_ssem.at[to], q_rsem.at[z], where
+            ),
+            remote(end_send, end_recv.at[z], end_ssem.at[to], end_rsem.at[z], where),
+        )
+
+    for to in range(last):
+
+        @pl.when(to < z)
+        def _():
+            for copy in ask(to):
+                copy.start()
+
+    @pl.when(z == last - 1)
+    def _():
+        keep_state()
+
+    def hop(h, p, src):
+        piece = pl.ds(p * part_rows, part_rows)
+        return remote(
+            src.at[h, piece],
+            state_in.at[h, piece],
+            chain_send.at[h, p],
+            chain_recv.at[h, p],
+            {"seq": z + 1},
+        )
+
+    def set_off(which):
+        @pl.when((z == 0) & (z < last))
+        def _():
+            for h in which:
+                for p in range(PARTS):
+                    hop(h, p, own_state).start()
+
+    lead = heads - heads // 4
+    ahead = max(lead - max(last - 1, 0), 0)
+    set_off(range(ahead))
+
+    @pl.when(z == last)
+    def _():
+        inputs["k"].wait()
+        inputs["v"].wait()
+
+    for h in range(heads):
+        cols = slice(h * hd, (h + 1) * hd)
+        scores = nt_dot(q_ref[:, cols], k_ref[:, cols])
+        gaps = cum[:, h : h + 1] - cum_t[h : h + 1, :]
+        mixing = jnp.where(causal, scores * jnp.exp(jnp.where(causal, gaps, 0.0)), 0.0)
+        att[:, cols] = jnp.dot(mixing.astype(BF16), v_ref[:, cols], preferred_element_type=F32)
+
+    for name in ("res", "gate", "again", "mgain", "rw"):
+        inputs[name].wait()
+    near_att = pick(att[...].astype(BF16))
+    near_res = pick(res_ref[...])
+    near_v = jax.nn.sigmoid(pick(gate_ref[...])) * again_ref[...]
+    near[0] = near_att
+    near[1] = near_v
+    near[2] = near_res
+
+    spot = lax.broadcasted_iota(jnp.int32, (picked, 128), 1)
+
+    def peer_of(i):
+        to = lax.rem(me + 1 + i, peers)
+        return {"exp": lax.div(to, n_rep), "rep": lax.rem(to, n_rep)}
+
+    def products(attended, gated, residual):
+        u = gated * attended
+        parts = (attended * attended, residual * u, u * u, residual * residual)
+        return u, [jnp.sum(part, axis=1, keepdims=True) for part in parts]
+
+    def first_tell(i):
+        return remote(
+            first_sums.at[me], first_sums.at[me], first_ssem, first_rsem, peer_of(i)
+        )
+
+    @pl.when(z == 0)
+    def _():
+        _, wholes = products(near_att, near_v, near_res)
+        table = jnp.zeros((picked, 128), F32)
+        for n, whole in enumerate(wholes):
+            table = jnp.where(spot == n, whole, table)
+        first_sums[me] = table
+        for i in range(peers - 1):
+            first_tell(i).start()
+
+    def to_home(i):
+        return remote(
+            extra_send.at[i, :, used],
+            extra_recv.at[i, :, used],
+            extra_ssem.at[i],
+            extra_rsem.at[i],
+            {"seq": middle},
+        )
+
+    @pl.when(z > 0)
+    def _():
+        put(res_pack, near_res * mgain_ref[...])
+        res_rows[r, here] = res_pack[x]
+
+    if middle != last:
+
+        @pl.when(z == last)
+        def _():
+            for i, value in enumerate((near_att, near_v, near_res)):
+                put(extra_send.at[i], value)
+                to_home(i).start()
+
+    def own_line(send, order=None):
+        for i in order or [n for k in range(n_seq) for n in (last - k, k)][:n_seq]:
+
+            @pl.when(i != z)
+            def _():
+                send(x, i)
+
+    def other_lines(send, order=None):
+        for j in range(1, n_exp):
+            for i in order or [n for k in range(n_seq) for n in (last - k, k)][:n_seq]:
+                send(lax.rem(x + j, n_exp), i)
+
+    def send_res(e, to):
+        remote(
+            res_pack.at[e, used],
+            res_rows.at[r, here, used],
+            res_ssem,
+            res_rsem,
+            {"exp": e, "seq": to},
+        ).start()
+
+    def keep(b, i):
+        rows[r, x * n_seq + b] = pack[i, x]
+
+    def spread(b, i):
+        spot_of = x * n_seq + b
+
+        def send(e, to):
+            remote(
+                pack.at[i, e, used],
+                rows.at[r, spot_of, used],
+                disp_send,
+                disp_recv,
+                {"exp": e, "seq": to},
+            ).start()
+
+        return send
+
+    def hand_out(b, i, attended, gated, residual):
+        u, wholes = products(attended, gated, residual)
+        table = jnp.zeros((picked, 128), F32)
+        for n, whole in enumerate(wholes):
+            coarse = whole.astype(BF16).astype(F32)
+            table = jnp.where(spot == n, coarse, table)
+            table = jnp.where(spot == n + len(wholes), whole - coarse, table)
+        put(pack.at[i], u * mgain_ref[...])
+        for e in range(n_exp):
+            pack[i, e, :, columns:] = table[e * SLOTS : (e + 1) * SLOTS, :].astype(BF16)
+        keep(b, i)
+        return spread(b, i)
+
+    def norms(total):
+        s1 = lax.rsqrt(total[0] / width + EPSILON)
+        moe = total[3] + s1 * (2.0 * total[1] + s1 * total[2])
+        return s1, lax.rsqrt(jnp.maximum(moe, 0.0) / width + EPSILON)
+
+    @pl.when(z > 0)
+    def _():
+        own_line(send_res)
+        pl.semaphore_wait(go_sem, n_exp - 1)
+        other_lines(send_res)
+
+    def offer(b):
+        target = tail_recv if b == last else part_recv
+        return remote(
+            part_send.at[b, :, used],
+            target.at[z, :, used],
+            part_ssem.at[b],
+            part_rsem.at[1 if b == last else 0, z],
+            {"seq": home(b)},
+        )
+
+    def relay(h):
+        cols = slice(h * hd, (h + 1) * hd)
+        for p in range(PARTS):
+            piece = slice(p * part_rows, (p + 1) * part_rows)
+            hop(h, p, state_out).wait_recv()
+
+            @pl.when(z < last)
+            def _():
+                state_out[h, piece] = (
+                    fading[:, h : h + 1] * state_in[h, piece].astype(F32)
+                    + block_state[h, piece]
+                ).astype(BF16)
+                hop(h, p, state_out).start()
+
+        att[:, cols] += jnp.dot(lifted[:, cols], state_in[h], preferred_element_type=F32)
+
+    def relays(where, which):
+        @pl.when(where)
+        def _():
+            for h in which:
+                relay(h)
+
+    chained = (z > 0) & (z < last)
+    for b in range(1, n_seq):
+
+        @pl.when(z < b)
+        def _():
+            ask_q = remote(q_send.at[:, used], q_recv.at[b, :, used], q_ssem.at[0], q_rsem.at[b], {"seq": 0})
+            ask_e = remote(end_send, end_recv.at[b], end_ssem.at[0], end_rsem.at[b], {"seq": 0})
+            ask_q.wait_recv()
+            ask_e.wait_recv()
+            between = jnp.zeros((1, 128), F32)
+            for m in range(1, b):
+                between += jnp.where(m > z, end_recv[m], 0.0)
+            between = jnp.exp(between)
+            asked = take(q_recv.at[b]).astype(BF16)
+            given = [
+                jnp.dot(
+                    asked[:, h * hd : (h + 1) * hd], own_state[h], preferred_element_type=F32
+                )
+                * between[:, h : h + 1]
+                for h in range(heads)
+            ]
+            given = jnp.concatenate(given, axis=1)
+            put(part_send.at[b], given)
+
+            @pl.when(z != home(b))
+            def _():
+                offer(b).start()
+
+            if b == last:
+
+                @pl.when(z == home(b))
+                def _():
+                    put(tail_recv.at[z], given)
+
+        if b < last:
+            set_off(range(ahead + b - 1, min(ahead + b, lead)))
+
+    @pl.when(z == 0)
+    def _():
+        let_go()
+
+    @pl.when(z == 0)
+    def _():
+        everyone = first_sums.at[pl.ds(0, peers - 1)]
+        pltpu.make_async_copy(everyone, everyone, first_rsem).wait()
+        total = jnp.sum(first_sums[...], axis=0)
+        s1, s2 = norms([total[:, n : n + 1] for n in range(4)])
+        normed = (near[2] + s1 * (near[0] * near[1])) * s2 * mgain_ref[...]
+        put(pack.at[0], normed)
+        keep(0, 0)
+        own_line(spread(0, 0))
+
+        pl.semaphore_wait(go_sem, n_exp - 1)
+        other_lines(spread(0, 0))
+
+    set_off(range(lead, heads))
+
+    def wait_part(which, source):
+        buffer = tail_recv if which else part_recv
+        remote(
+            part_send.at[0, :, used],
+            buffer.at[source, :, used],
+            part_ssem.at[0],
+            part_rsem.at[which, source],
+            {"seq": 0},
+        ).wait_recv()
+
+    @pl.when((z > 0) & (z < last))
+    def _():
+        acc[...] = near[0]
+        for source in range(last):
+
+            @pl.when(source < z)
+            def _():
+                wait_part(0, source)
+                acc[...] += take(part_recv.at[source])
+
+        send = hand_out(z, 0, acc[...], near[1], near[2])
+        own_line(send)
+        other_lines(send)
+
+    relays(chained & (z == 1), range(ahead))
+
+    @pl.when(z == middle)
+    def _():
+        for i in range(3):
+            to_home(i).wait_recv()
+        whole = take(extra_recv.at[0])
+        whole += take(tail_recv.at[middle])
+        for source in range(last):
+            if source != middle:
+                wait_part(1, source)
+                whole += take(tail_recv.at[source])
+        send = hand_out(last, 1, whole, take(extra_recv.at[1]), take(extra_recv.at[2]))
+        order = sorted(range(n_seq), key=lambda i: -abs(i - middle))
+        own_line(send, order)
+        other_lines(send, order)
+
+    relays(chained & (z == 1), range(ahead, lead))
+
+    slots = n_seq * SLOTS
+
+    def project(table, s):
+        gate_part = up_part = 0.0
+        for e in range(n_exp):
+            chunk = table[s, pl.ds(e * n_seq, n_seq)].astype(F32)[:, :, 0:columns]
+            chunk = chunk.reshape(slots, columns).astype(BF16)
+            at = pl.ds(pl.multiple_of((e * n_rep + s) * columns, 128), columns)
+            gate_part += nt_dot(wg[:, at], chunk)
+            up_part += nt_dot(wu[:, at], chunk)
+        return gate_part, up_part
+
+    def swap(table, i):
+        return remote(
+            table.at[r], table.at[r], swap_send.at[i], swap_recv.at[i], {"rep": other}
+        )
+
+    res_sent = res_rows.at[r, pl.ds(0, plane - 1), used]
+    for n in range(2):
+
+        @pl.when(jnp.where(z > 0, 1, 0) == n)
+        def _():
+            arrived = res_rows.at[r, pl.ds(0, plane - n_exp - n), used]
+            pltpu.make_async_copy(arrived, arrived, res_rsem).wait()
+
+    swap(res_rows, 0).start()
+    for load in loads:
+        load.wait()
+    gate_val, up_val = project(res_rows, r)
+    swap(res_rows, 0).wait()
+    gate_part, up_part = project(res_rows, other)
+    gate_early[...] = gate_val + gate_part
+    up_early[...] = up_val + up_part
+
+    relays(chained & (z == 1), range(lead, heads))
+    relays(chained & (z > 1), range(ahead))
+
+    mine = jnp.where(z < last, 1, 0) + jnp.where(z == middle, 1, 0)
+    for n in range(3):
+
+        @pl.when(mine == n)
+        def _():
+            arrived = rows.at[r, pl.ds(0, plane - n), used]
+            pltpu.make_async_copy(arrived, arrived, disp_recv).wait()
+
+    swap(rows, 1).start()
+    gate_val, up_val = project(rows, r)
+    relays(chained & (z > 1), range(ahead, lead))
+    swap(rows, 1).wait()
+    gate_part, up_part = project(rows, other)
+    table = 0.0
+    for s in range(n_rep):
+        for e in range(n_exp):
+            table += rows[s, pl.ds(e * n_seq, n_seq)].astype(F32)[:, :, columns:]
+    table = jnp.transpose(table.reshape(slots, 128))
+    total = table[0:4, :] + table[4:8, :]
+    s1, s2 = norms([total[n : n + 1, :] for n in range(4)])
+    whole = lax.broadcasted_iota(jnp.int32, (hidden_rows, slots), 1) < SLOTS
+    gate_b, up_b = gate_val + gate_part, up_val + up_part
+    gate_val = jnp.where(whole, gate_b, s2 * (gate_early[...] + s1 * gate_b))
+    up_val = jnp.where(whole, up_b, s2 * (up_early[...] + s1 * up_b))
+    inner = gate_val / (1.0 + jnp.exp(-gate_val)) * up_val
+    if hidden_rows == whole_rows:
+        unit = lax.broadcasted_iota(jnp.int32, inner.shape, 0)
+        inner = jnp.where(lax.div(unit, whole_rows // n_rep) == r, inner, 0.0)
+    inner = jnp.transpose(inner).astype(BF16)
+    relays(chained & (z > 1), range(lead, heads))
+
+    def product(e, s):
+        at = pl.multiple_of((e * n_rep + s) * columns, 128)
+        return jnp.dot(inner, wd[:, pl.ds(at, columns)], preferred_element_type=F32)
+
+    def half(e):
+        return remote(
+            half_send.at[e], half_recv.at[e], half_ssem.at[e], half_rsem.at[e], {"rep": other}
+        )
+
+    for e in range(n_exp):
+        half_send[e] = product(e, other).astype(BF16)
+        half(e).start()
+
+    for e in range(n_exp):
+        own = product(e, r)
+        half(e).wait_recv()
+        whole = (own + half_recv[e].astype(F32)).reshape(n_seq, SLOTS, columns)
+        fin[pl.ds(e * n_seq, n_seq)] = whole.astype(BF16)
+
+    back[here] = fin[here]
+
+    def hand_back(e, to):
+        remote(
+            fin.at[e * n_seq + to, used],
+            back.at[here, used],
+            back_send,
+            back_recv,
+            {"exp": e, "seq": to},
+        ).start()
+
+    other_lines(hand_back)
+    own_line(hand_back)
+
+    relays((z > 0) & (z == last), range(heads))
+    attended = att[...]
+    square = jnp.sum(attended * attended, axis=1, keepdims=True)
+    table = jnp.where(lane == 0, square, 0.0)
+    sums[me] = jnp.transpose(table)[0:8, :]
+
+    def tell(i):
+        return remote(sums.at[me], sums.at[me], sums_send, sums_recv, peer_of(i))
+
+    for i in range(peers - 1):
+        tell(i).start()
+    u_buf[...] = jax.nn.sigmoid(gate_ref[...].astype(F32)) * attended * again_ref[...]
+    shares = jnp.transpose(rw_ref[...])
+    combine = jnp.where(first_hit, shares[:, 0:1], shares[:, 1:2]) * onehot
+    coarse = combine.astype(BF16)
+    fine = (combine - coarse.astype(F32)).astype(BF16)
+
+    for to in range(last):
+
+        @pl.when(to < z)
+        def _():
+            for copy in ask(to):
+                copy.wait_send()
+
+    if middle != last:
+
+        @pl.when(z == last)
+        def _():
+            for i in range(3):
+                to_home(i).wait_send()
+
+    for b in range(1, n_seq):
+
+        @pl.when((z < b) & (z != home(b)))
+        def _():
+            offer(b).wait_send()
+
+    @pl.when(z < last)
+    def _():
+        for h in range(heads):
+            for p in range(PARTS):
+                hop(h, p, state_out).wait_send()
+
+    @pl.when(z > 0)
+    def _():
+        pltpu.make_async_copy(res_sent, res_sent, res_ssem).wait()
+
+    @pl.when(z == 0)
+    def _():
+        everyone = first_sums.at[pl.ds(0, peers - 1)]
+        pltpu.make_async_copy(everyone, everyone, first_ssem).wait()
+
+    for n in range(1, 3):
+
+        @pl.when(mine == n)
+        def _():
+            for _ in range(n):
+                sent = rows.at[r, pl.ds(0, plane - 1), used]
+                pltpu.make_async_copy(sent, sent, disp_send).wait()
+
+    for e in range(n_exp):
+        half(e).wait_send()
+
+    many = sums.at[pl.ds(0, peers - 1)]
+    pltpu.make_async_copy(many, many, sums_recv).wait()
+    total = jnp.sum(sums[...], axis=0)
+    scale = lax.rsqrt(total / width + EPSILON)
+    scale = jnp.transpose(scale)[:, 0:1]
+    u_buf[...] = res_ref[...].astype(F32) + scale * u_buf[...]
+    pltpu.make_async_copy(many, many, sums_send).wait()
+
+    returned = back.at[pl.ds(0, plane - 1), used]
+    pltpu.make_async_copy(returned, returned, back_recv).wait()
+    result = u_buf[...]
+    for e in range(n_exp):
+        rows_e = jnp.sum(back[pl.ds(e * n_seq, n_seq)].astype(F32), axis=0)
+        slot = lax.broadcasted_iota(jnp.int32, rows_e.shape, 0)
+        rows_e = jnp.where(slot < CAP, rows_e, 0.0).astype(BF16)
+        lanes = slice(e * SLOTS, (e + 1) * SLOTS)
+        result += jnp.dot(coarse[:, lanes], rows_e, preferred_element_type=F32)
+        result += jnp.dot(fine[:, lanes], rows_e, preferred_element_type=F32)
+    out_ref[...] = result.astype(BF16)
+    pltpu.make_async_copy(returned, returned, back_send).wait()
+
+
 def solution(mesh):
     n_seq, n_exp, n_rep = (mesh.shape[a] for a in ("seq", "exp", "rep"))
 
@@ -456,8 +1189,106 @@
         vmem = pl.BlockSpec(memory_space=pltpu.VMEM)
         hbm = pl.BlockSpec(memory_space=pltpu.HBM)
         dma = pltpu.SemaphoreType.DMA
+        if 2 < n_seq <= SHORT:
+            wide = columns + 128
+            return pl.pallas_call(
+                lambda *refs: direct_kernel(n_seq, n_exp, n_rep, *refs),
+                name="layer",
+                out_shape=pltpu.VMEM((tokens, columns), BF16),
+                in_specs=[hbm] * 13,
+                out_specs=vmem,
+                scratch_shapes=[
+                    pltpu.VMEM((tokens, columns), BF16),
+                    pltpu.VMEM((tokens, columns), BF16),
+                    pltpu.VMEM((heads, tokens), F32),
+                    pltpu.VMEM((tokens, columns), BF16),
+                    pltpu.VMEM((2, tokens), jnp.int32),
+                    pltpu.VMEM((2, tokens), F32),
+                    pltpu.VMEM((tokens, columns), BF16),
+                    pltpu.VMEM((tokens, columns), BF16),
+                    pltpu.VMEM((1, columns), F32),
+                    pltpu.VMEM((1, columns), F32),
+                    pltpu.VMEM((hidden_rows, width), BF16),
+                    pltpu.VMEM((hidden_rows, width), BF16),
+                    pltpu.VMEM((hidden_rows, width), BF16),
+                    pltpu.VMEM((heads, hd, hd), BF16),
+                    pltpu.VMEM((heads, hd, hd), BF16),
+                    pltpu.VMEM((heads, hd, hd), BF16),
+                    pltpu.VMEM((heads, hd, hd), F32),
+                    pltpu.VMEM((tokens, columns), BF16),
+                    pltpu.VMEM((tokens, columns), F32),
+                    pltpu.VMEM((tokens, columns), F32),
+                    pltpu.VMEM((n_exp * n_rep, 8, tokens), F32),
+                    pltpu.VMEM((n_exp * n_rep, n_exp * SLOTS, 128), F32),
+                    pltpu.VMEM((1, 128), F32),
+                    pltpu.VMEM((n_seq, 1, 128), F32),
+                    pltpu.VMEM((n_exp, SLOTS, columns), BF16),
+                    pltpu.VMEM((n_seq, n_exp, SLOTS, columns), BF16),
+                    pltpu.VMEM((n_seq, n_exp, SLOTS, columns), BF16),
+                    pltpu.VMEM((n_seq, n_exp, SLOTS, columns), BF16),
+                    pltpu.VMEM((n_seq, n_exp, SLOTS, columns), BF16),
+                    pltpu.VMEM((3, n_exp, SLOTS, columns), BF16),
+                    pltpu.VMEM((3, n_exp, SLOTS, columns), BF16),
+                    pltpu.VMEM((3, n_exp * SLOTS, columns), F32),
+                    pltpu.VMEM((n_exp * SLOTS, columns), F32),
+                    pltpu.VMEM((n_exp, SLOTS, columns), BF16),
+                    pltpu.VMEM((n_rep, plane, SLOTS, columns), BF16),
+                    pltpu.VMEM((2, n_exp, SLOTS, wide), BF16),
+                    pltpu.VMEM((n_rep, plane, SLOTS, wide), BF16),
+                    pltpu.VMEM((hidden_rows, slots), F32),
+                    pltpu.VMEM((hidden_rows, slots), F32),
+                    pltpu.VMEM((n_exp, slots, columns), BF16),
+                    pltpu.VMEM((n_exp, slots, columns), BF16),
+                    pltpu.VMEM((plane, SLOTS, columns), BF16),
+                    pltpu.VMEM((plane, SLOTS, columns), BF16),
+                    dma((10,)),
+                    dma((3,)),
+                    pltpu.SemaphoreType.REGULAR,
+                    dma((heads, PARTS)),
+                    dma((heads, PARTS)),
+                    dma,
+                    dma,
+                    dma,
+                    dma,
+                    dma((n_seq,)),
+                    dma((n_seq,)),
+                    dma((n_seq,)),
+                    dma((n_seq,)),
+                    dma((n_seq,)),
+                    dma((2, n_seq)),
+                    dma((3,)),
+                    dma((3,)),
+                    dma,
+                    dma,
+                    dma,
+                    dma,
+                    dma((2,)),
+                    dma((2,)),
+                    dma((n_exp,)),
+                    dma((n_exp,)),
+                    dma,
+                    dma,
+                ],
+                compiler_params=pltpu.CompilerParams(
+                    collective_id=0, has_side_effects=True, vmem_limit_bytes=63000000
+                ),
+            )(
+                key_rows,
+                value_rows,
+                decay_log.T,
+                queries,
+                routes.T,
+                route_weights.T,
+                residual,
+                out_gate,
+                attn_gain.reshape(1, columns),
+                moe_gain.reshape(1, columns),
+                w_gate,
+                w_up,
+                w_down,
+            )
         return pl.pallas_call(
-            lambda *refs: kernel(n_seq, n_exp, n_rep, *refs),
+            lambda *refs: chain_kernel(n_seq, n_exp, n_rep, *refs),
             name="layer",
             out_shape=pltpu.VMEM((tokens, columns), BF16),
             in_specs=[hbm] * 13,

time: 34.2 us -> 31.2 us (0.912)
  Pallas kernels: 33.4 us -> 30.4 us
    pallas_call x1, Pallas kernels: 33.4 us -> 30.4 us  [shards(): pl.pallas_call(lambda *refs: direct_kernel(n_seq, n_exp, n_rep, *refs), n...]
where the time goes in v2:
time: 31.2 us; the launch traced here: 31.1 us
  Pallas kernels  30.4 us (97%)
  local copies, waits for them, and re-layouts  0.66 us (2%)
    pallas_call x1, Pallas kernels, shards(): pl.pallas_call(lambda *refs: direct_kernel(n_seq, n_exp, n_rep, *refs), n...  30.4 us
    unnamed x1, local copies, waits for them, and re-layouts  0.66 us

profile of v2, /device:TPU:0, one launch (start us, length us, event | category | flops | bytes accessed | tf_op | source)
XLA Modules:
  0.0 31.1 jit_solution(3173694158265248524)
XLA Ops:
  0.0 30.4 %layer.1 = bf16[64,1024]{1,0:T(8,128)(2,1)S(1)} custom-call(bf16[64,1024]{1,0:T(8,128)(2,1)} %refs_0_.1, bf16[64,1024]{1,0:T(8,128)(2,1)} %refs_1_.1, f32[8,64]{1,0:T(8,128)} %bitcast.5, bf16[64,1024]{1,0:T(8,128)(2,1)} %refs_3_.1, s32[2,64]{1,0:T(2,128)} %bitcast.8, f32[2,64]{1,0:T(2,128)} %bitcast.9, bf16[64,1024]{1,0:T(8,128)(2,1)} %refs_6_.1, ...), custom_call_target="tpu_custom_call" | custom-call | tf_op jit(solution)/shard_map/layer/pallas_call | solution.py:1194
  30.4 0.7 %copy.15 = bf16[64,1024]{1,0:T(8,128)(2,1)} copy(bf16[64,1024]{1,0:T(8,128)(2,1)S(1)} %layer.1) | data formatting | bytes 262144

commit v3 on v2

--- a/solution.py
+++ b/solution.py
@@ -479,6 +479,7 @@
     extra_recv,
     near,
     acc,
+    fade,
     res_pack,
     res_rows,
     pack,
@@ -603,7 +604,7 @@
     )
     cum = jnp.transpose(cum_t)
     ending = cum[tokens - 1 : tokens, :]
-    fading = jnp.exp(ending)
+    fade[...] = jnp.broadcast_to(jnp.exp(cum_t[:, tokens - 1 : tokens]), fade.shape)
     to_end = jnp.exp(ending - cum)
     lift = jnp.exp(cum)
     end_send[...] = jnp.zeros(end_send.shape, F32)
@@ -708,7 +709,7 @@
                     hop(h, p, own_state).start()
 
     lead = heads - heads // 4
-    ahead = max(lead - max(last - 1, 0), 0)
+    ahead = heads // 2
     set_off(range(ahead))
 
     @pl.when(z == last)
@@ -853,20 +854,13 @@
         )
 
     def relay(h):
-        cols = slice(h * hd, (h + 1) * hd)
         for p in range(PARTS):
             piece = slice(p * part_rows, (p + 1) * part_rows)
             hop(h, p, state_out).wait_recv()
-
-            @pl.when(z < last)
-            def _():
-                state_out[h, piece] = (
-                    fading[:, h : h + 1] * state_in[h, piece].astype(F32)
-                    + block_state[h, piece]
-                ).astype(BF16)
-                hop(h, p, state_out).start()
-
-        att[:, cols] += jnp.dot(lifted[:, cols], state_in[h], preferred_element_type=F32)
+            state_out[h, piece] = (
+                fade[h : h + 1, :] * state_in[h, piece].astype(F32) + block_state[h, piece]
+            ).astype(BF16)
+            hop(h, p, state_out).start()
 
     def relays(where, which):
         @pl.when(where)
@@ -908,12 +902,11 @@
                 def _():
                     put(tail_recv.at[z], given)
 
-        if b < last:
-            set_off(range(ahead + b - 1, min(ahead + b, lead)))
-
     @pl.when(z == 0)
     def _():
         let_go()
+
+    relays(chained & (z == 1), range(ahead))
 
     @pl.when(z == 0)
     def _():
@@ -926,6 +919,10 @@
         keep(0, 0)
         own_line(spread(0, 0))
 
+    set_off(range(ahead, lead))
+
+    @pl.when(z == 0)
+    def _():
         pl.semaphore_wait(go_sem, n_exp - 1)
         other_lines(spread(0, 0))
 
@@ -955,7 +952,6 @@
         own_line(send)
         other_lines(send)
 
-    relays(chained & (z == 1), range(ahead))
 
     @pl.when(z == middle)
     def _():
@@ -1075,7 +1071,20 @@
     other_lines(hand_back)
     own_line(hand_back)
 
-    relays((z > 0) & (z == last), range(heads))
+    @pl.when(z == last)
+    def _():
+        for h in range(heads):
+            for p in range(PARTS):
+                hop(h, p, state_out).wait_recv()
+
+    @pl.when(z > 0)
+    def _():
+        for h in range(heads):
+            cols = slice(h * hd, (h + 1) * hd)
+            att[:, cols] += jnp.dot(
+                lifted[:, cols], state_in[h], preferred_element_type=F32
+            )
+
     attended = att[...]
     square = jnp.sum(attended * attended, axis=1, keepdims=True)
     table = jnp.where(lane == 0, square, 0.0)
@@ -1231,6 +1240,7 @@
                     pltpu.VMEM((3, n_exp, SLOTS, columns), BF16),
                     pltpu.VMEM((3, n_exp * SLOTS, columns), F32),
                     pltpu.VMEM((n_exp * SLOTS, columns), F32),
+                    pltpu.VMEM((heads, 128), F32),
                     pltpu.VMEM((n_exp, SLOTS, columns), BF16),
                     pltpu.VMEM((n_rep, plane, SLOTS, columns), BF16),
                     pltpu.VMEM((2, n_exp, SLOTS, wide), BF16),

time: 31.2 us -> 29.2 us (0.936)
  Pallas kernels: 30.4 us -> 28.3 us
    pallas_call x1, Pallas kernels: 30.4 us -> 28.3 us  [shards(): pl.pallas_call(lambda *refs: direct_kernel(n_seq, n_exp, n_rep, *refs), n...]
where the time goes in v3:
time: 29.2 us; the launch traced here: 29 us
  Pallas kernels  28.3 us (97%)
  local copies, waits for them, and re-layouts  0.66 us (2%)
    pallas_call x1, Pallas kernels, shards(): pl.pallas_call(lambda *refs: direct_kernel(n_seq, n_exp, n_rep, *refs), n...  28.3 us
    unnamed x1, local copies, waits for them, and re-layouts  0.66 us

profile of v3, /device:TPU:0, one launch (start us, length us, event | category | flops | bytes accessed | tf_op | source)
XLA Modules:
  0.0 29.0 jit_solution(6026111612565451081)
XLA Ops:
  0.0 28.3 %layer.1 = bf16[64,1024]{1,0:T(8,128)(2,1)S(1)} custom-call(bf16[64,1024]{1,0:T(8,128)(2,1)} %refs_0_.1, bf16[64,1024]{1,0:T(8,128)(2,1)} %refs_1_.1, f32[8,64]{1,0:T(8,128)} %bitcast.5, bf16[64,1024]{1,0:T(8,128)(2,1)} %refs_3_.1, s32[2,64]{1,0:T(2,128)} %bitcast.8, f32[2,64]{1,0:T(2,128)} %bitcast.9, bf16[64,1024]{1,0:T(8,128)(2,1)} %refs_6_.1, ...), custom_call_target="tpu_custom_call" | custom-call | tf_op jit(solution)/shard_map/layer/pallas_call | solution.py:1203
  28.3 0.7 %copy.15 = bf16[64,1024]{1,0:T(8,128)(2,1)} copy(bf16[64,1024]{1,0:T(8,128)(2,1)S(1)} %layer.1) | data formatting | bytes 262144

commit v4 on v3

--- a/solution.py
+++ b/solution.py
@@ -484,10 +484,8 @@
     res_rows,
     pack,
     rows,
-    gate_early,
-    up_early,
-    half_send,
-    half_recv,
+    inner_head,
+    inner_tail,
     fin,
     back,
     in_sem,
@@ -513,8 +511,8 @@
     disp_recv,
     swap_send,
     swap_recv,
-    half_ssem,
-    half_rsem,
+    inner_ssem,
+    inner_rsem,
     back_send,
     back_recv,
 ):
@@ -528,7 +526,7 @@
     part_rows = hd // PARTS
     hidden_rows = wg.shape[0]
     width = columns * n_exp * n_rep
-    whole_rows = wg_hbm.shape[1]
+    cut = inner_head.shape[2]
     plane = n_exp * n_seq
     peers = n_exp * n_rep
     me = x * n_rep + r
@@ -576,11 +574,16 @@
         to = lax.rem(me + 1 + i, peers)
         greet({"exp": lax.div(to, n_rep), "rep": lax.rem(to, n_rep)})
 
-    first = pl.multiple_of(r * hidden_rows, 16) if hidden_rows != whole_rows else 0
+    first = pl.ds(pl.multiple_of(r * hidden_rows, 16), hidden_rows)
     loads = [
-        pltpu.make_async_copy(src.at[0, pl.ds(first, hidden_rows), :], dst, w_sem.at[i])
-        for i, (src, dst) in enumerate(((wg_hbm, wg), (wu_hbm, wu), (wd_hbm, wd)))
+        pltpu.make_async_copy(src.at[0, first, :], dst, w_sem.at[i])
+        for i, (src, dst) in enumerate(((wg_hbm, wg), (wu_hbm, wu)))
     ]
+    for e in range(n_exp):
+        at = pl.ds(pl.multiple_of((e * n_rep + r) * columns, 128), columns)
+        loads.append(
+            pltpu.make_async_copy(wd_hbm.at[0, :, at], wd.at[e], w_sem.at[len(loads)])
+        )
     for load in loads:
         load.start()
 
@@ -595,6 +598,7 @@
         )
 
     inputs["decay"].wait()
+    inputs["routes"].wait()
     ti = lax.broadcasted_iota(jnp.int32, (tokens, tokens), 0)
     tj = lax.broadcasted_iota(jnp.int32, (tokens, tokens), 1)
     causal = ti >= tj
@@ -609,7 +613,6 @@
     lift = jnp.exp(cum)
     end_send[...] = jnp.zeros(end_send.shape, F32)
     end_send[:, 0:heads] = ending
-    inputs["routes"].wait()
     lane = lax.broadcasted_iota(jnp.int32, (tokens, 128), 1)
     expert_of = lax.div(lane, SLOTS)
     slot_of = lax.rem(lane, SLOTS)
@@ -680,12 +683,15 @@
             remote(end_send, end_recv.at[z], end_ssem.at[to], end_rsem.at[z], where),
         )
 
-    for to in range(last):
-
-        @pl.when(to < z)
-        def _():
-            for copy in ask(to):
-                copy.start()
+    def asks(which):
+        for to in which:
+
+            @pl.when(to < z)
+            def _():
+                for copy in ask(to):
+                    copy.start()
+
+    asks(range(1))
 
     @pl.when(z == last - 1)
     def _():
@@ -708,14 +714,16 @@
                 for p in range(PARTS):
                     hop(h, p, own_state).start()
 
-    lead = heads - heads // 4
-    ahead = heads // 2
-    set_off(range(ahead))
+    quarter = heads // 4
+    lead = heads - quarter
+    set_off(range(lead))
 
     @pl.when(z == last)
     def _():
         inputs["k"].wait()
         inputs["v"].wait()
+
+    asks(range(1, last))
 
     for h in range(heads):
         cols = slice(h * hd, (h + 1) * hd)
@@ -837,11 +845,14 @@
         moe = total[3] + s1 * (2.0 * total[1] + s1 * total[2])
         return s1, lax.rsqrt(jnp.maximum(moe, 0.0) / width + EPSILON)
 
-    @pl.when(z > 0)
-    def _():
+    def send_all_res():
         own_line(send_res)
         pl.semaphore_wait(go_sem, n_exp - 1)
         other_lines(send_res)
+
+    @pl.when((z > 0) & (z != last - 1))
+    def _():
+        send_all_res()
 
     def offer(b):
         target = tail_recv if b == last else part_recv
@@ -906,7 +917,13 @@
     def _():
         let_go()
 
-    relays(chained & (z == 1), range(ahead))
+    if last > 1:
+
+        @pl.when(z == last - 1)
+        def _():
+            send_all_res()
+
+    relays(chained & (z == 1), range(quarter))
 
     @pl.when(z == 0)
     def _():
@@ -918,8 +935,6 @@
         put(pack.at[0], normed)
         keep(0, 0)
         own_line(spread(0, 0))
-
-    set_off(range(ahead, lead))
 
     @pl.when(z == 0)
     def _():
@@ -968,18 +983,27 @@
         own_line(send, order)
         other_lines(send, order)
 
-    relays(chained & (z == 1), range(ahead, lead))
-
     slots = n_seq * SLOTS
 
-    def project(table, s):
+    def pair(s, e):
+        return jnp.concatenate(
+            [
+                table[s, pl.ds(e * n_seq, n_seq)]
+                .astype(F32)[:, :, 0:columns]
+                .reshape(slots, columns)
+                .astype(BF16)
+                for table in (rows, res_rows)
+            ],
+            axis=0,
+        )
+
+    def project(s, lines):
         gate_part = up_part = 0.0
         for e in range(n_exp):
-            chunk = table[s, pl.ds(e * n_seq, n_seq)].astype(F32)[:, :, 0:columns]
-            chunk = chunk.reshape(slots, columns).astype(BF16)
+            chunk = pair(s, e)
             at = pl.ds(pl.multiple_of((e * n_rep + s) * columns, 128), columns)
-            gate_part += nt_dot(wg[:, at], chunk)
-            up_part += nt_dot(wu[:, at], chunk)
+            gate_part += nt_dot(wg[lines, at], chunk)
+            up_part += nt_dot(wu[lines, at], chunk)
         return gate_part, up_part
 
     def swap(table, i):
@@ -996,16 +1020,10 @@
             pltpu.make_async_copy(arrived, arrived, res_rsem).wait()
 
     swap(res_rows, 0).start()
+    relays(chained & (z == 1), range(quarter, heads))
+    relays(chained & (z > 1), range(quarter))
     for load in loads:
         load.wait()
-    gate_val, up_val = project(res_rows, r)
-    swap(res_rows, 0).wait()
-    gate_part, up_part = project(res_rows, other)
-    gate_early[...] = gate_val + gate_part
-    up_early[...] = up_val + up_part
-
-    relays(chained & (z == 1), range(lead, heads))
-    relays(chained & (z > 1), range(ahead))
 
     mine = jnp.where(z < last, 1, 0) + jnp.where(z == middle, 1, 0)
     for n in range(3):
@@ -1016,46 +1034,55 @@
             pltpu.make_async_copy(arrived, arrived, disp_recv).wait()
 
     swap(rows, 1).start()
-    gate_val, up_val = project(rows, r)
-    relays(chained & (z > 1), range(ahead, lead))
+    gate_own, up_own = project(r, slice(0, hidden_rows))
+    relays(chained & (z > 1), range(quarter, 2 * quarter))
+    swap(res_rows, 0).wait()
     swap(rows, 1).wait()
-    gate_part, up_part = project(rows, other)
     table = 0.0
     for s in range(n_rep):
         for e in range(n_exp):
             table += rows[s, pl.ds(e * n_seq, n_seq)].astype(F32)[:, :, columns:]
-    table = jnp.transpose(table.reshape(slots, 128))
-    total = table[0:4, :] + table[4:8, :]
-    s1, s2 = norms([total[n : n + 1, :] for n in range(4)])
-    whole = lax.broadcasted_iota(jnp.int32, (hidden_rows, slots), 1) < SLOTS
-    gate_b, up_b = gate_val + gate_part, up_val + up_part
-    gate_val = jnp.where(whole, gate_b, s2 * (gate_early[...] + s1 * gate_b))
-    up_val = jnp.where(whole, up_b, s2 * (up_early[...] + s1 * up_b))
-    inner = gate_val / (1.0 + jnp.exp(-gate_val)) * up_val
-    if hidden_rows == whole_rows:
-        unit = lax.broadcasted_iota(jnp.int32, inner.shape, 0)
-        inner = jnp.where(lax.div(unit, whole_rows // n_rep) == r, inner, 0.0)
-    inner = jnp.transpose(inner).astype(BF16)
+    table = table.reshape(slots, 128)
+    s1, s2 = norms([table[:, n : n + 1] + table[:, n + 4 : n + 5] for n in range(4)])
+    whole = lax.broadcasted_iota(jnp.int32, (slots, 1), 0) < SLOTS
+
+    def scaled(values):
+        values = jnp.transpose(values)
+        fresh = values[0:slots, :]
+        return jnp.where(whole, fresh, s2 * (values[slots:, :] + s1 * fresh))
+
+    def share(i):
+        part = (inner_head, inner_tail)[i]
+        return remote(
+            part.at[r], part.at[r], inner_ssem.at[i], inner_rsem.at[i], {"rep": other}
+        )
+
+    for i, lines in enumerate((slice(0, cut), slice(cut, hidden_rows))):
+        gate_part, up_part = project(other, lines)
+        gate_val = scaled(gate_own[lines] + gate_part)
+        up_val = scaled(up_own[lines] + up_part)
+        inner = gate_val / (1.0 + jnp.exp(-gate_val)) * up_val
+        (inner_head, inner_tail)[i][r] = inner.astype(BF16)
+        share(i).start()
+
+    relays(chained & (z > 1), range(2 * quarter, lead))
+
+    def product(e, s):
+        start = s * hidden_rows
+        head = pl.ds(pl.multiple_of(start, 16), cut)
+        tail = pl.ds(pl.multiple_of(start + cut, 16), hidden_rows - cut)
+        return jnp.dot(
+            inner_head[s], wd[e, head, :], preferred_element_type=F32
+        ) + jnp.dot(inner_tail[s], wd[e, tail, :], preferred_element_type=F32)
+
+    halves = [product(e, r) for e in range(n_exp)]
+    for i in range(2):
+        share(i).wait_recv()
+    for e in range(n_exp):
+        both = (halves[e] + product(e, other)).reshape(n_seq, SLOTS, columns)
+        fin[pl.ds(e * n_seq, n_seq)] = both.astype(BF16)
+
     relays(chained & (z > 1), range(lead, heads))
-
-    def product(e, s):
-        at = pl.multiple_of((e * n_rep + s) * columns, 128)
-        return jnp.dot(inner, wd[:, pl.ds(at, columns)], preferred_element_type=F32)
-
-    def half(e):
-        return remote(
-            half_send.at[e], half_recv.at[e], half_ssem.at[e], half_rsem.at[e], {"rep": other}
-        )
-
-    for e in range(n_exp):
-        half_send[e] = product(e, other).astype(BF16)
-        half(e).start()
-
-    for e in range(n_exp):
-        own = product(e, r)
-        half(e).wait_recv()
-        whole = (own + half_recv[e].astype(F32)).reshape(n_seq, SLOTS, columns)
-        fin[pl.ds(e * n_seq, n_seq)] = whole.astype(BF16)
 
     back[here] = fin[here]
 
@@ -1071,6 +1098,7 @@
     other_lines(hand_back)
     own_line(hand_back)
 
+
     @pl.when(z == last)
     def _():
         for h in range(heads):
@@ -1144,8 +1172,8 @@
                 sent = rows.at[r, pl.ds(0, plane - 1), used]
                 pltpu.make_async_copy(sent, sent, disp_send).wait()
 
-    for e in range(n_exp):
-        half(e).wait_send()
+    for i in range(2):
+        share(i).wait_send()
 
     many = sums.at[pl.ds(0, peers - 1)]
     pltpu.make_async_copy(many, many, sums_recv).wait()
@@ -1198,7 +1226,8 @@
         vmem = pl.BlockSpec(memory_space=pltpu.VMEM)
         hbm = pl.BlockSpec(memory_space=pltpu.HBM)
         dma = pltpu.SemaphoreType.DMA
-        if 2 < n_seq <= SHORT:
+        cut = hidden_rows // 256 * 128
+        if 2 < n_seq <= SHORT and even and cut > 0:
             wide = columns + 128
             return pl.pallas_call(
                 lambda *refs: direct_kernel(n_seq, n_exp, n_rep, *refs),
@@ -1219,7 +1248,7 @@
                     pltpu.VMEM((1, columns), F32),
                     pltpu.VMEM((hidden_rows, width), BF16),
                     pltpu.VMEM((hidden_rows, width), BF16),
-                    pltpu.VMEM((hidden_rows, width), BF16),
+                    pltpu.VMEM((n_exp, whole_rows, columns), BF16),
                     pltpu.VMEM((heads, hd, hd), BF16),
                     pltpu.VMEM((heads, hd, hd), BF16),
                     pltpu.VMEM((heads, hd, hd), BF16),
@@ -1245,14 +1274,12 @@
                     pltpu.VMEM((n_rep, plane, SLOTS, columns), BF16),
                     pltpu.VMEM((2, n_exp, SLOTS, wide), BF16),
                     pltpu.VMEM((n_rep, plane, SLOTS, wide), BF16),
-                    pltpu.VMEM((hidden_rows, slots), F32),
-                    pltpu.VMEM((hidden_rows, slots), F32),
-                    pltpu.VMEM((n_exp, slots, columns), BF16),
-                    pltpu.VMEM((n_exp, slots, columns), BF16),
+                    pltpu.VMEM((n_rep, slots, cut), BF16),
+                    pltpu.VMEM((n_rep, slots, hidden_rows - cut), BF16),
                     pltpu.VMEM((plane, SLOTS, columns), BF16),
                     pltpu.VMEM((plane, SLOTS, columns), BF16),
                     dma((10,)),
-                    dma((3,)),
+                    dma((2 + n_exp,)),
                     pltpu.SemaphoreType.REGULAR,
                     dma((heads, PARTS)),
                     dma((heads, PARTS)),
@@ -1274,8 +1301,8 @@
                     dma,
                     dma((2,)),
                     dma((2,)),
-                    dma((n_exp,)),
-                    dma((n_exp,)),
+                    dma((2,)),
+                    dma((2,)),
                     dma,
                     dma,
                 ],

time: 29.2 us -> 28.6 us (0.979)
  Pallas kernels: 28.3 us -> 27.8 us
    pallas_call x1, Pallas kernels: 28.3 us -> 27.8 us  [shards(): pl.pallas_call(lambda *refs: direct_kernel(n_seq, n_exp, n_rep, *refs), n...]
where the time goes in v4:
time: 28.6 us; the launch traced here: 28.5 us
  Pallas kernels  27.8 us (97%)
  local copies, waits for them, and re-layouts  0.66 us (2%)
    pallas_call x1, Pallas kernels, shards(): pl.pallas_call(lambda *refs: direct_kernel(n_seq, n_exp, n_rep, *refs), n...  27.8 us
    unnamed x1, local copies, waits for them, and re-layouts  0.66 us

profile of v4, /device:TPU:0, one launch (start us, length us, event | category | flops | bytes accessed | tf_op | source)
XLA Modules:
  0.0 28.5 jit_solution(15150727186584718891)
XLA Ops:
  0.0 27.8 %layer.1 = bf16[64,1024]{1,0:T(8,128)(2,1)S(1)} custom-call(bf16[64,1024]{1,0:T(8,128)(2,1)} %refs_0_.1, bf16[64,1024]{1,0:T(8,128)(2,1)} %refs_1_.1, f32[8,64]{1,0:T(8,128)} %bitcast.5, bf16[64,1024]{1,0:T(8,128)(2,1)} %refs_3_.1, s32[2,64]{1,0:T(2,128)} %bitcast.8, f32[2,64]{1,0:T(2,128)} %bitcast.9, bf16[64,1024]{1,0:T(8,128)(2,1)} %refs_6_.1, ...), custom_call_target="tpu_custom_call" | custom-call | tf_op jit(solution)/shard_map/layer/pallas_call | solution.py:1232
  27.8 0.7 %copy.15 = bf16[64,1024]{1,0:T(8,128)(2,1)} copy(bf16[64,1024]{1,0:T(8,128)(2,1)S(1)} %layer.1) | data formatting | bytes 262144

commit v5 on v4

--- a/solution.py
+++ b/solution.py
@@ -531,7 +531,7 @@
     peers = n_exp * n_rep
     me = x * n_rep + r
     last = n_seq - 1
-    middle = last // 2
+    middle = max(last - 1, 0)
     picked = n_exp * SLOTS
     used = pl.ds(0, CAP)
     here = x * n_seq + z
@@ -673,7 +673,6 @@
     def _():
         let_go()
 
-
     def ask(to):
         where = {"seq": to}
         return (
@@ -821,7 +820,7 @@
                 pack.at[i, e, used],
                 rows.at[r, spot_of, used],
                 disp_send,
-                disp_recv,
+                disp_recv.at[b],
                 {"exp": e, "seq": to},
             ).start()
 
@@ -850,7 +849,7 @@
         pl.semaphore_wait(go_sem, n_exp - 1)
         other_lines(send_res)
 
-    @pl.when((z > 0) & (z != last - 1))
+    @pl.when(z > 0)
     def _():
         send_all_res()
 
@@ -917,12 +916,6 @@
     def _():
         let_go()
 
-    if last > 1:
-
-        @pl.when(z == last - 1)
-        def _():
-            send_all_res()
-
     relays(chained & (z == 1), range(quarter))
 
     @pl.when(z == 0)
@@ -967,6 +960,8 @@
         own_line(send)
         other_lines(send)
 
+
+    relays(chained & (z == 1), range(quarter, 2 * quarter))
 
     @pl.when(z == middle)
     def _():
@@ -1020,22 +1015,24 @@
             pltpu.make_async_copy(arrived, arrived, res_rsem).wait()
 
     swap(res_rows, 0).start()
-    relays(chained & (z == 1), range(quarter, heads))
-    relays(chained & (z > 1), range(quarter))
+    relays(chained & (z == 1), range(2 * quarter, heads))
+    relays(chained & (z > 1), range(lead // 2))
     for load in loads:
         load.wait()
 
     mine = jnp.where(z < last, 1, 0) + jnp.where(z == middle, 1, 0)
-    for n in range(3):
-
-        @pl.when(mine == n)
-        def _():
-            arrived = rows.at[r, pl.ds(0, plane - n), used]
-            pltpu.make_async_copy(arrived, arrived, disp_recv).wait()
+    for b in range(n_seq):
+        for own in range(2):
+
+            @pl.when(jnp.where(z == home(b), 1, 0) == own)
+            def _():
+                if n_exp - own > 0:
+                    arrived = rows.at[r, pl.ds(0, n_exp - own), used]
+                    pltpu.make_async_copy(arrived, arrived, disp_recv.at[b]).wait()
 
     swap(rows, 1).start()
     gate_own, up_own = project(r, slice(0, hidden_rows))
-    relays(chained & (z > 1), range(quarter, 2 * quarter))
+    relays(chained & (z > 1), range(lead // 2, lead))
     swap(res_rows, 0).wait()
     swap(rows, 1).wait()
     table = 0.0
@@ -1065,26 +1062,12 @@
         (inner_head, inner_tail)[i][r] = inner.astype(BF16)
         share(i).start()
 
-    relays(chained & (z > 1), range(2 * quarter, lead))
-
-    def product(e, s):
-        start = s * hidden_rows
-        head = pl.ds(pl.multiple_of(start, 16), cut)
-        tail = pl.ds(pl.multiple_of(start + cut, 16), hidden_rows - cut)
-        return jnp.dot(
-            inner_head[s], wd[e, head, :], preferred_element_type=F32
-        ) + jnp.dot(inner_tail[s], wd[e, tail, :], preferred_element_type=F32)
-
-    halves = [product(e, r) for e in range(n_exp)]
-    for i in range(2):
-        share(i).wait_recv()
-    for e in range(n_exp):
-        both = (halves[e] + product(e, other)).reshape(n_seq, SLOTS, columns)
-        fin[pl.ds(e * n_seq, n_seq)] = both.astype(BF16)
-
     relays(chained & (z > 1), range(lead, heads))
 
-    back[here] = fin[here]
+    def product(e, s, i):
+        part = (inner_head, inner_tail)[i]
+        lines = pl.ds(pl.multiple_of(s * hidden_rows + i * cut, 16), part.shape[2])
+        return jnp.dot(part[s], wd[e, lines, :], preferred_element_type=F32)
 
     def hand_back(e, to):
         remote(
@@ -1095,10 +1078,20 @@
             {"exp": e, "seq": to},
         ).start()
 
-    other_lines(hand_back)
+    turns = [lax.rem(x + j, n_exp) for j in range(1, n_exp + 1)]
+    totals = [product(e, r, 0) + product(e, r, 1) for e in turns]
+    share(0).wait_recv()
+    totals = [total + product(e, other, 0) for total, e in zip(totals, turns)]
+    share(1).wait_recv()
+    for n, (total, e) in enumerate(zip(totals, turns)):
+        whole = (total + product(e, other, 1)).reshape(n_seq, SLOTS, columns)
+        fin[pl.ds(e * n_seq, n_seq)] = whole.astype(BF16)
+        if n < n_exp - 1:
+            for i in [n for k in range(n_seq) for n in (last - k, k)][:n_seq]:
+                hand_back(e, i)
+
+    back[here] = fin[here]
     own_line(hand_back)
-
-
     @pl.when(z == last)
     def _():
         for h in range(heads):
@@ -1298,7 +1291,7 @@
                     dma,
                     dma,
                     dma,
-                    dma,
+                    dma((n_seq,)),
                     dma((2,)),
                     dma((2,)),
                     dma((2,)),

time: 28.6 us -> 28.2 us (0.986)
  Pallas kernels: 27.8 us -> 27.4 us
    pallas_call x1, Pallas kernels: 27.8 us -> 27.4 us  [shards(): pl.pallas_call(lambda *refs: direct_kernel(n_seq, n_exp, n_rep, *refs), n...]
where the time goes in v5:
time: 28.2 us; the launch traced here: 28.1 us
  Pallas kernels  27.4 us (97%)
  local copies, waits for them, and re-layouts  0.66 us (2%)
    pallas_call x1, Pallas kernels, shards(): pl.pallas_call(lambda *refs: direct_kernel(n_seq, n_exp, n_rep, *refs), n...  27.4 us
    unnamed x1, local copies, waits for them, and re-layouts  0.66 us

profile of v5, /device:TPU:0, one launch (start us, length us, event | category | flops | bytes accessed | tf_op | source)
XLA Modules:
  0.0 28.1 jit_solution(100421602328534680)
XLA Ops:
  0.0 27.4 %layer.1 = bf16[64,1024]{1,0:T(8,128)(2,1)S(1)} custom-call(bf16[64,1024]{1,0:T(8,128)(2,1)} %refs_0_.1, bf16[64,1024]{1,0:T(8,128)(2,1)} %refs_1_.1, f32[8,64]{1,0:T(8,128)} %bitcast.5, bf16[64,1024]{1,0:T(8,128)(2,1)} %refs_3_.1, s32[2,64]{1,0:T(2,128)} %bitcast.8, f32[2,64]{1,0:T(2,128)} %bitcast.9, bf16[64,1024]{1,0:T(8,128)(2,1)} %refs_6_.1, ...), custom_call_target="tpu_custom_call" | custom-call | tf_op jit(solution)/shard_map/layer/pallas_call | solution.py:1225
  27.4 0.7 %copy.15 = bf16[64,1024]{1,0:T(8,128)(2,1)} copy(bf16[64,1024]{1,0:T(8,128)(2,1)S(1)} %layer.1) | data formatting | bytes 262144

commit v6 on v5

--- a/solution.py
+++ b/solution.py
@@ -1016,7 +1016,7 @@
 
     swap(res_rows, 0).start()
     relays(chained & (z == 1), range(2 * quarter, heads))
-    relays(chained & (z > 1), range(lead // 2))
+    relays(chained & (z > 1), range(quarter))
     for load in loads:
         load.wait()
 
@@ -1032,7 +1032,7 @@
 
     swap(rows, 1).start()
     gate_own, up_own = project(r, slice(0, hidden_rows))
-    relays(chained & (z > 1), range(lead // 2, lead))
+    relays(chained & (z > 1), range(quarter, lead - 1))
     swap(res_rows, 0).wait()
     swap(rows, 1).wait()
     table = 0.0
@@ -1062,7 +1062,7 @@
         (inner_head, inner_tail)[i][r] = inner.astype(BF16)
         share(i).start()
 
-    relays(chained & (z > 1), range(lead, heads))
+    relays(chained & (z > 1), range(lead - 1, heads))
 
     def product(e, s, i):
         part = (inner_head, inner_tail)[i]
@@ -1074,7 +1074,7 @@
             fin.at[e * n_seq + to, used],
             back.at[here, used],
             back_send,
-            back_recv,
+            back_recv.at[here],
             {"exp": e, "seq": to},
         ).start()
 
@@ -1087,11 +1087,11 @@
         whole = (total + product(e, other, 1)).reshape(n_seq, SLOTS, columns)
         fin[pl.ds(e * n_seq, n_seq)] = whole.astype(BF16)
         if n < n_exp - 1:
-            for i in [n for k in range(n_seq) for n in (last - k, k)][:n_seq]:
+            for i in range(n_seq):
                 hand_back(e, i)
 
     back[here] = fin[here]
-    own_line(hand_back)
+    own_line(hand_back, range(n_seq))
     @pl.when(z == last)
     def _():
         for h in range(heads):
@@ -1177,7 +1177,13 @@
     pltpu.make_async_copy(many, many, sums_send).wait()
 
     returned = back.at[pl.ds(0, plane - 1), used]
-    pltpu.make_async_copy(returned, returned, back_recv).wait()
+    for spot_of in [e * n_seq + n for n in range(n_seq) for e in range(n_exp)]:
+
+        @pl.when(spot_of != here)
+        def _():
+            one = back.at[spot_of, used]
+            pltpu.make_async_copy(one, one, back_recv.at[spot_of]).wait()
+
     result = u_buf[...]
     for e in range(n_exp):
         rows_e = jnp.sum(back[pl.ds(e * n_seq, n_seq)].astype(F32), axis=0)
@@ -1297,7 +1303,7 @@
                     dma((2,)),
                     dma((2,)),
                     dma,
-                    dma,
+                    dma((plane,)),
                 ],
                 compiler_params=pltpu.CompilerParams(
                     collective_id=0, has_side_effects=True, vmem_limit_bytes=63000000

time: 28.2 us -> 28 us (level)
  Pallas kernels: 27.4 us -> 27.1 us
where the time goes in v6:
time: 28 us; the launch traced here: 27.8 us
  Pallas kernels  27.1 us (97%)
  local copies, waits for them, and re-layouts  0.66 us (2%)
    pallas_call x1, Pallas kernels, shards(): pl.pallas_call(lambda *refs: direct_kernel(n_seq, n_exp, n_rep, *refs), n...  27.1 us
    unnamed x1, local copies, waits for them, and re-layouts  0.66 us

profile of v6, /device:TPU:0, one launch (start us, length us, event | category | flops | bytes accessed | tf_op | source)
XLA Modules:
  0.0 27.8 jit_solution(8756207848986411583)
XLA Ops:
  0.0 27.1 %layer.1 = bf16[64,1024]{1,0:T(8,128)(2,1)S(1)} custom-call(bf16[64,1024]{1,0:T(8,128)(2,1)} %refs_0_.1, bf16[64,1024]{1,0:T(8,128)(2,1)} %refs_1_.1, f32[8,64]{1,0:T(8,128)} %bitcast.5, bf16[64,1024]{1,0:T(8,128)(2,1)} %refs_3_.1, s32[2,64]{1,0:T(2,128)} %bitcast.8, f32[2,64]{1,0:T(2,128)} %bitcast.9, bf16[64,1024]{1,0:T(8,128)(2,1)} %refs_6_.1, ...), custom_call_target="tpu_custom_call" | custom-call | tf_op jit(solution)/shard_map/layer/pallas_call | solution.py:1231
  27.1 0.7 %copy.15 = bf16[64,1024]{1,0:T(8,128)(2,1)} copy(bf16[64,1024]{1,0:T(8,128)(2,1)S(1)} %layer.1) | data formatting | bytes 262144

commit v7 on v6

--- a/solution.py
+++ b/solution.py
@@ -961,8 +961,6 @@
         other_lines(send)
 
 
-    relays(chained & (z == 1), range(quarter, 2 * quarter))
-
     @pl.when(z == middle)
     def _():
         for i in range(3):
@@ -1015,7 +1013,7 @@
             pltpu.make_async_copy(arrived, arrived, res_rsem).wait()
 
     swap(res_rows, 0).start()
-    relays(chained & (z == 1), range(2 * quarter, heads))
+    relays(chained & (z == 1), range(quarter, heads))
     relays(chained & (z > 1), range(quarter))
     for load in loads:
         load.wait()
@@ -1184,14 +1182,18 @@
             one = back.at[spot_of, used]
             pltpu.make_async_copy(one, one, back_recv.at[spot_of]).wait()
 
+    slot = lax.rem(lax.broadcasted_iota(jnp.int32, (picked, columns), 0), SLOTS)
+    owed = jnp.concatenate(
+        [
+            jnp.sum(back[pl.ds(e * n_seq, n_seq)].astype(F32), axis=0)
+            for e in range(n_exp)
+        ],
+        axis=0,
+    )
+    owed = jnp.where(slot < CAP, owed, 0.0).astype(BF16)
     result = u_buf[...]
-    for e in range(n_exp):
-        rows_e = jnp.sum(back[pl.ds(e * n_seq, n_seq)].astype(F32), axis=0)
-        slot = lax.broadcasted_iota(jnp.int32, rows_e.shape, 0)
-        rows_e = jnp.where(slot < CAP, rows_e, 0.0).astype(BF16)
-        lanes = slice(e * SLOTS, (e + 1) * SLOTS)
-        result += jnp.dot(coarse[:, lanes], rows_e, preferred_element_type=F32)
-        result += jnp.dot(fine[:, lanes], rows_e, preferred_element_type=F32)
+    for part in (coarse, fine):
+        result += jnp.dot(part[:, 0:picked], owed, preferred_element_type=F32)
     out_ref[...] = result.astype(BF16)
     pltpu.make_async_copy(returned, returned, back_send).wait()
 
@@ -1225,7 +1227,7 @@
         vmem = pl.BlockSpec(memory_space=pltpu.VMEM)
         hbm = pl.BlockSpec(memory_space=pltpu.HBM)
         dma = pltpu.SemaphoreType.DMA
-        cut = hidden_rows // 256 * 128
+        cut = hidden_rows // 192 * 128
         if 2 < n_seq <= SHORT and even and cut > 0:
             wide = columns + 128
             return pl.pallas_call(

time: 28 us -> 27.8 us (level)
  no operation moved by 1% of the time
where the time goes in v7:
time: 27.8 us; the launch traced here: 27.7 us
  Pallas kernels  27 us (97%)
  local copies, waits for them, and re-layouts  0.66 us (2%)
    pallas_call x1, Pallas kernels, shards(): pl.pallas_call(lambda *refs: direct_kernel(n_seq, n_exp, n_rep, *refs), n...  27 us
    unnamed x1, local copies, waits for them, and re-layouts  0.66 us

profile of v7, /device:TPU:0, one launch (start us, length us, event | category | flops | bytes accessed | tf_op | source)
XLA Modules:
  0.0 27.7 jit_solution(16722541747185211861)
XLA Ops:
  0.0 27.0 %layer.1 = bf16[64,1024]{1,0:T(8,128)(2,1)S(1)} custom-call(bf16[64,1024]{1,0:T(8,128)(2,1)} %refs_0_.1, bf16[64,1024]{1,0:T(8,128)(2,1)} %refs_1_.1, f32[8,64]{1,0:T(8,128)} %bitcast.5, bf16[64,1024]{1,0:T(8,128)(2,1)} %refs_3_.1, s32[2,64]{1,0:T(2,128)} %bitcast.8, f32[2,64]{1,0:T(2,128)} %bitcast.9, bf16[64,1024]{1,0:T(8,128)(2,1)} %refs_6_.1, ...), custom_call_target="tpu_custom_call" | custom-call | tf_op jit(solution)/shard_map/layer/pallas_call | solution.py:1233
  27.0 0.7 %copy.15 = bf16[64,1024]{1,0:T(8,128)(2,1)} copy(bf16[64,1024]{1,0:T(8,128)(2,1)S(1)} %layer.1) | data formatting | bytes 262144

commit v8 on v7

--- a/solution.py
+++ b/solution.py
@@ -957,8 +957,8 @@
                 acc[...] += take(part_recv.at[source])
 
         send = hand_out(z, 0, acc[...], near[1], near[2])
+        other_lines(send)
         own_line(send)
-        other_lines(send)
 
 
     @pl.when(z == middle)
@@ -973,8 +973,8 @@
                 whole += take(tail_recv.at[source])
         send = hand_out(last, 1, whole, take(extra_recv.at[1]), take(extra_recv.at[2]))
         order = sorted(range(n_seq), key=lambda i: -abs(i - middle))
+        other_lines(send, order)
         own_line(send, order)
-        other_lines(send, order)
 
     slots = n_seq * SLOTS
 

time: 27.8 us -> 27.8 us (level)
  no operation moved by 1% of the time
where the time goes in v8:
time: 27.8 us; the launch traced here: 27.7 us
  Pallas kernels  27 us (97%)
  local copies, waits for them, and re-layouts  0.66 us (2%)
    pallas_call x1, Pallas kernels, shards(): pl.pallas_call(lambda *refs: direct_kernel(n_seq, n_exp, n_rep, *refs), n...  27 us
    unnamed x1, local copies, waits for them, and re-layouts  0.66 us

profile of v8, /device:TPU:0, one launch (start us, length us, event | category | flops | bytes accessed | tf_op | source)
XLA Modules:
  0.0 27.7 jit_solution(4637583300393745581)
XLA Ops:
  0.0 27.0 %layer.1 = bf16[64,1024]{1,0:T(8,128)(2,1)S(1)} custom-call(bf16[64,1024]{1,0:T(8,128)(2,1)} %refs_0_.1, bf16[64,1024]{1,0:T(8,128)(2,1)} %refs_1_.1, f32[8,64]{1,0:T(8,128)} %bitcast.5, bf16[64,1024]{1,0:T(8,128)(2,1)} %refs_3_.1, s32[2,64]{1,0:T(2,128)} %bitcast.8, f32[2,64]{1,0:T(2,128)} %bitcast.9, bf16[64,1024]{1,0:T(8,128)(2,1)} %refs_6_.1, ...), custom_call_target="tpu_custom_call" | custom-call | tf_op jit(solution)/shard_map/layer/pallas_call | solution.py:1233
  27.0 0.7 %copy.15 = bf16[64,1024]{1,0:T(8,128)(2,1)} copy(bf16[64,1024]{1,0:T(8,128)(2,1)S(1)} %layer.1) | data formatting | bytes 262144
